TPU v7x, 128 devices: a whole 4x4x4 slice. The times are simulated.
128 devices in a mesh: dp: 1, tp: 2 (over core), ep: 64 (over z, y, x).
Axes of the slice: x: 4, y: 4, z: 4, core: 2. Of those that a mesh axis runs over, the one named last changes fastest.
Arguments:
- act_in: bfloat16 [262144, 768], P(('dp', 'ep'))
- expert_idx: int32 [262144, 1], P(('dp', 'ep'))
- gate_vals: float32 [262144, 1], P(('dp', 'ep'))
- w_in: bfloat16 [64, 768, 3072], P('ep', None, 'tp')
- w_out: bfloat16 [64, 3072, 768], P('ep', 'tp')
Outputs:
- output: bfloat16 [262144, 768], P(('dp', 'ep'))
All inputs are finite; a program needn't handle non-finite values.
Results may differ from a plain program's by a relative error of at most 0.001.
Values are sent between devices in bfloat16 or wider.
A program may use at most 1 GiB of HBM per device.

v0:
```python
import jax
import jax.numpy as jnp
from jax import lax
from jax.sharding import PartitionSpec as P, NamedSharding


def capacity_of(top_k, tokens, experts, tp_size):
    divisor = 32 * experts * tp_size
    return 8 * tp_size * ((5 * top_k * tokens + divisor - 1) // divisor)


def route_slots(idx_loc, experts):
    hit_mask = idx_loc[:, :, None] == jnp.arange(experts)[None, None, :]
    per_tok = jnp.sum(hit_mask, axis=1, dtype=jnp.int32)
    preceding = jnp.cumsum(per_tok, axis=0) - per_tok
    return jnp.sum(jnp.where(hit_mask, preceding[:, None, :], 0), axis=2)


def solution(mesh):
    tp_size = mesh.shape["tp"]
    ep_size = mesh.shape["ep"]

    def local_moe(act_loc, idx_loc, gate_loc, w_in, w_out):
        tokens, hidden = act_loc.shape
        top_k = idx_loc.shape[1]
        local_experts = w_in.shape[0]
        experts = local_experts * ep_size
        capacity = capacity_of(top_k, tokens, experts, tp_size)
        slot_width = capacity // tp_size
        slot_ids = route_slots(idx_loc, experts)
        group_of = idx_loc // local_experts
        local_of = idx_loc % local_experts
        own_slot = slot_ids - lax.axis_index("tp") * slot_width
        is_sent = (own_slot >= 0) & (own_slot < slot_width)
        n_send = experts * slot_width
        send_pos = jnp.where(is_sent, (local_of * ep_size + group_of) * slot_width + own_slot, n_send).reshape(-1)
        tok_ids = jnp.broadcast_to(jnp.arange(tokens, dtype=jnp.int32)[:, None], idx_loc.shape).reshape(-1)
        tok_table = jnp.full((n_send + 1,), tokens, jnp.int32).at[send_pos].set(tok_ids)[:n_send]
        outgoing = jnp.take(act_loc, tok_table, axis=0, mode="fill", fill_value=0).reshape(local_experts, ep_size, slot_width, hidden)
        arrived = lax.all_to_all(outgoing, "ep", 1, 1, tiled=True)
        expert_in = lax.all_gather(arrived, "tp", axis=2, tiled=True)
        pre_act = jnp.einsum("escd,edf->escf", expert_in, w_in, preferred_element_type=jnp.float32)
        hidden_act = jax.nn.gelu(pre_act, approximate=True).astype(jnp.bfloat16)
        part_out = jnp.einsum("escf,efd->escd", hidden_act, w_out, preferred_element_type=jnp.float32)
        expert_out = lax.psum_scatter(part_out, "tp", scatter_dimension=2, tiled=True).astype(jnp.bfloat16)
        returned = lax.all_to_all(expert_out, "ep", 1, 1, tiled=True)
        own_out = lax.all_gather(returned, "tp", axis=2, tiled=True).reshape(experts * capacity, hidden)
        out_pos = jnp.where(slot_ids < capacity, (local_of * ep_size + group_of) * capacity + slot_ids, experts * capacity)
        picked = jnp.take(own_out, out_pos, axis=0, mode="fill", fill_value=0)
        combined = jnp.sum(gate_loc[:, :, None] * picked, axis=1)
        return combined.astype(jnp.bfloat16)

    tok_spec = P(("dp", "ep"), None)
    return jax.shard_map(local_moe, mesh=mesh, in_specs=(tok_spec, tok_spec, tok_spec, P("ep", None, "tp"), P("ep", "tp", None)), out_specs=tok_spec, check_vma=False)
```

profile of v0, /device:TPU:41, one launch (start us, length us, event | category | flops | bytes accessed | tf_op | source)
XLA Modules:
  0.0 357.0 jit_solution(4805342094655575296)
XLA Ops:
  6.5 0.0 copy-start
  6.5 0.0 all-gather.3.cloned.1.call-start
  6.5 2.0 fusion.25
  8.5 32.3 %reduce-window.6 = s32[64,32,128]{2,1,0:T(8,128)S(1)} reduce-window(s32[64,32,128]{2,1,0:T(8,128)} %fusion.25, s32[]{:T(128)} %constant.44.clone.1), window={size=1x1x128 pad=0_0x0_0x127_0}, to_apply=%region_0.0 | reduce-window | flops 33292288 | bytes 2097156 | tf_op jit(solution)/shard_map/reduce-window
  40.8 1.3 slice.19
  42.1 1.7 copy.13
  43.8 0.2 reduce-window.9
  44.0 1.3 broadcast_add_fusion
  45.3 0.0 copy-done.2
  45.3 2.2 fusion.24
  47.6 15.5 %scatter_custom_fusion = s32[2561]{0:T(1024)S(1)} fusion(s32[4096]{0:T(1024)S(1)} %bitcast.63, s32[4096]{0:T(1024)S(1)} %iota.13, s32[]{:T(128)} %constant.48.clone.1), kind=kCustom, calls=%fused_computation.39 | custom fusion | bytes 10248 | tf_op jit(solution)/shard_map/scatter | solution.py:38
  63.1 0.1 slice.14
  63.2 13.9 %gather_fusion = bf16[2560,768]{1,0:T(8,128)(2,1)} fusion(bf16[4096,768]{1,0:T(8,128)(2,1)} %param.5, s32[3072]{0:T(1024)S(1)} %pad_clamp_fusion), kind=kCustom, calls=%fused_computation | custom fusion | bytes 7874560 | tf_op jit(solution)/shard_map/jit(_take)/gather | solution.py:39
  77.1 2.4 broadcast_select_fusion
  79.5 65.3 %all_to_all.10 = bf16[1,64,40,768]{3,2,0,1:T(8,128)(2,1)} all-to-all(bf16[1,64,40,768]{3,2,0,1:T(8,128)(2,1)S(1)} %broadcast_select_fusion), channel_id=1, replica_groups=mesh['dp'=1,'tp'=2,'ep'=64] {'ep'}, dimensions={1} | all-to-all | bytes 7864320 | tf_op jit(solution)/shard_map/all_to_all | solution.py:40
  144.8 0.0 all-gather.3.cloned.1.call-update
  144.8 0.0 reduce-scatter.2.cloned.1.call-start
  144.9 24.5 %all-gather.3.cloned.1.call-done = bf16[1,64,80,768]{3,2,1,0:T(8,128)(2,1)} async-done(((bf16[1,64,40,768]{3,2,1,0:T(8,128)(2,1)}), bf16[1,64,80,768]{3,2,1,0:T(8,128)(2,1)}) %all-gather.3.cloned.1.call-update) | async-done | bytes 7864336 | tf_op jit(solution)/shard_map/all_gather | solution.py:41
  169.4 0.0 copy-done
  169.4 33.7 %fusion.10 = f32[1,64,80,768]{3,2,1,0:T(8,128)} fusion(bf16[1,64,80,768]{3,2,1,0:T(8,128)(2,1)} %all-gather.3.cloned.1.call-done, bf16[1,1536,768]{2,1,0:T(8,128)(2,1)S(1)} %copy-done, bf16[1,768,1536]{2,1,0:T(8,128)(2,1)} %param.8), kind=kOutput, calls=%fused_computation.14 | convolution fusion | flops 24229969920 | bytes 28311552 | tf_op jit(solution)/shard_map/escf,efd->escd/dot_general | solution.py:44
  203.2 0.0 reduce-scatter.2.cloned.1.call-update
  203.2 0.0 all-gather.5.cloned.1.call-start
  203.2 24.8 %reduce-scatter.2.cloned.1.call-done = f32[1,64,40,768]{3,2,1,0:T(8,128)} async-done(((f32[1,64,80,768]{3,2,1,0:T(8,128)}), f32[1,64,40,768]{3,2,1,0:T(8,128)}) %reduce-scatter.2.cloned.1.call-update) | async-done | bytes 7864336 | tf_op jit(solution)/shard_map/reduce_scatter | solution.py:45
  228.0 3.6 %convert_bitcast_fusion = bf16[1,64,40,768]{3,2,0,1:T(8,128)(2,1)S(1)} fusion(f32[1,64,40,768]{3,2,1,0:T(8,128)} %reduce-scatter.2.cloned.1.call-done), kind=kLoop, calls=%fused_computation.17 | loop fusion | flops 1966080 | bytes 11796480 | tf_op jit(solution)/shard_map/convert_element_type | solution.py:45
  231.6 60.8 %all_to_all.11 = bf16[1,64,40,768]{3,2,0,1:T(8,128)(2,1)} all-to-all(bf16[1,64,40,768]{3,2,0,1:T(8,128)(2,1)S(1)} %convert_bitcast_fusion), channel_id=1, replica_groups=mesh['dp'=1,'tp'=2,'ep'=64] {'ep'}, dimensions={1} | all-to-all | bytes 7864320 | tf_op jit(solution)/shard_map/all_to_all | solution.py:46
  292.4 0.0 all-gather.5.cloned.1.call-update
  292.4 0.1 and_reduce_fusion
  292.6 26.6 %all-gather.5.cloned.1.call-done = bf16[1,64,80,768]{3,2,0,1:T(8,128)(2,1)} async-done(((bf16[1,64,40,768]{3,2,0,1:T(8,128)(2,1)}), bf16[1,64,80,768]{3,2,0,1:T(8,128)(2,1)}) %all-gather.5.cloned.1.call-update) | async-done | bytes 7864336 | tf_op jit(solution)/shard_map/all_gather | solution.py:47
  319.2 23.3 %gather_fusion.1 = bf16[4096,768]{1,0:T(8,128)(2,1)} fusion(bf16[5120,768]{1,0:T(8,128)(2,1)} %bitcast.51, s32[4096]{0:T(1024)S(1)} %broadcast_clamp_fusion), kind=kCustom, calls=%fused_computation.1 | custom fusion | bytes 12599296 | tf_op jit(solution)/shard_map/jit(_take)/gather | solution.py:49
  342.5 0.0 copy-done.3
  342.5 7.9 %multiply_convert_fusion = bf16[4096,768]{1,0:T(8,128)(2,1)} fusion(bf16[4096,768]{1,0:T(8,128)(2,1)} %gather_fusion.1, f32[4096]{0:T(1024)S(1)} %bitcast.62, pred[4096]{0:T(1024)(128)(4,1)S(1)} %get-tuple-element.5), kind=kLoop, calls=%fused_computation.13 | loop fusion | flops 12582912 | bytes 12603392 | tf_op jit(solution)/shard_map/convert_element_type | solution.py:51
  350.4 0.0 copy-done.1
  (9 shorter events, 0.1 us)
Async XLA Ops:
  6.5 162.9 %copy-start = (bf16[1,1536,768]{2,1,0:T(8,128)(2,1)S(1)}, bf16[1,1536,768]{2,1,0:T(8,128)(2,1)}, u32[]{:S(2)}) copy-start(bf16[1,1536,768]{2,1,0:T(8,128)(2,1)} %param.9) | copy-start | bytes 7077892
  6.5 38.8 %copy-start.2 = (s32[4096,1]{0,1:T(1,128)S(1)}, s32[4096,1]{0,1:T(1,128)}, u32[]{:S(2)}) copy-start(s32[4096,1]{0,1:T(1,128)} %param.6) | copy-start | bytes 49156
  6.5 162.9 %all-gather.3.cloned.1.call-start = ((), (), s32[]{:S(2)}) async-start(), calls=%async_computation.3 | async-start | bytes 11796480 | tf_op jit(solution)/shard_map/all_gather | solution.py:41
  144.8 83.2 %reduce-scatter.2.cloned.1.call-start = ((), (), s32[]{:S(2)}) async-start(), calls=%async_computation.4 | async-start | bytes 23592960 | tf_op jit(solution)/shard_map/reduce_scatter | solution.py:45
  203.2 116.0 %all-gather.5.cloned.1.call-start = ((), (), s32[]{:S(2)}) async-start(), calls=%async_computation.5 | async-start | bytes 11796480 | tf_op jit(solution)/shard_map/all_gather | solution.py:47
  319.2 23.3 %copy-start.3 = (f32[4096,1]{0,1:T(1,128)S(1)}, f32[4096,1]{0,1:T(1,128)}, u32[]{:S(2)}) copy-start(f32[4096,1]{0,1:T(1,128)} %param.7) | copy-start | bytes 49156
  342.5 7.9 %copy-start.1 = (bf16[1,1536,768]{2,1,0:T(8,128)(2,1)S(1)}, bf16[1,1536,768]{2,1,0:T(8,128)(2,1)}, u32[]{:S(2)}) copy-start(bf16[1,1536,768]{2,1,0:T(8,128)(2,1)} %param.9) | copy-start | bytes 7077892
Sparse Core Ops, SparseCore 0:
  144.9 24.4 all-gather.2
  203.3 24.6 reduce-scatter.1
  292.6 26.5 all-gather.4
where the time goes:
time: 361 us; the launch traced here: 357 us
  blocking collectives  126 us (35%)
  waiting for transfers between devices  76 us (21%)
  local copies, waits for them, and re-layouts  55.8 us (15%)
  other arithmetic  52.1 us (14%)
  matrix products  33.7 us (9%)
  between operations  13.2 us (4%)
    all_to_all x1, blocking collectives, local_moe(): arrived = lax.all_to_all(outgoing, 'ep', 1, 1, tiled=True)  65.3 us
    all_to_all x1, blocking collectives, local_moe(): returned = lax.all_to_all(expert_out, 'ep', 1, 1, tiled=True)  60.8 us
    another operation x3, other arithmetic  33.8 us
    dot_general x1, matrix products, local_moe(): jnp.einsum('escf,efd->escd', hidden_act, w_out, preferred_element_type=jn...  33.7 us
    all_gather x1, waiting for transfers between devices, local_moe(): lax.all_gather(returned, 'tp', axis=2, tiled=True)  26.6 us
    reduce_scatter x1, waiting for transfers between devices, local_moe(): lax.psum_scatter(part_out, 'tp', scatter_dimension=2, tiled=True)  24.8 us
    all_gather x1, waiting for transfers between devices, local_moe(): expert_in = lax.all_gather(arrived, 'tp', axis=2, tiled=True)  24.5 us
    gather x1, local copies, waits for them, and re-layouts, local_moe(): picked = jnp.take(own_out, out_pos, axis=0, mode='fill', fill_value=0)  23.3 us
  transfers between devices with their start and end apart: 3, of which 3 were waited for; matrix products, arithmetic and copies ran while one was open for 0% of the time, Pallas kernels for 0%

commit v1 on v0

v1 whole, which is shorter than its diff:
```python
import functools

import jax
import jax.numpy as jnp
from jax import lax
from jax.experimental import pallas as pl
from jax.experimental.pallas import tpu as pltpu
from jax.sharding import PartitionSpec as P

MESH = pl.DeviceIdType.MESH
SIDE = 4
CHIPS = SIDE ** 3
SUB = 8
LANES = 128


def capacity_of(top_k, tokens, experts, tp_size):
    divisor = 32 * experts * tp_size
    return 8 * tp_size * ((5 * top_k * tokens + divisor - 1) // divisor)


def my_coords():
    me = lax.axis_index("ep")
    return me % SIDE, (me // SIDE) % SIDE, me // (SIDE * SIDE)


def iota(shape, dim):
    return lax.broadcasted_iota(jnp.int32, shape, dim)


def route_kernel(cap, units, idx_ref, place_ref, table_ref, hits):
    blocks = idx_ref.shape[0]
    half = cap // 2
    expert_ids = iota((CHIPS, LANES), 0)
    for blk in range(blocks):
        hit = idx_ref[blk:blk + 1, :] == expert_ids
        hits[blk * CHIPS:(blk + 1) * CHIPS, :] = jnp.where(hit, 1.0, 0.0).astype(jnp.bfloat16)
    before = jnp.where(iota((LANES, LANES), 0) < iota((LANES, LANES), 1), 1.0, 0.0)
    mix = jnp.concatenate([before, jnp.ones((LANES, LANES), jnp.float32)], axis=1).astype(jnp.bfloat16)
    counts = jnp.dot(hits[...], mix, preferred_element_type=jnp.float32)
    base = jnp.zeros((CHIPS, LANES), jnp.float32)
    x, y, z = my_coords()
    high = jnp.zeros((CHIPS, cap), jnp.float32)
    low = jnp.zeros((CHIPS, cap), jnp.float32)
    slot_ids = iota((cap, LANES), 0)
    dims = (((1,), (1,)), ((), ()))
    for blk in range(blocks):
        rows = slice(blk * CHIPS, (blk + 1) * CHIPS)
        hit_b = hits[rows, :]
        rank = counts[rows, :LANES] + base
        slot_f = jnp.sum(hit_b.astype(jnp.float32) * rank, axis=0, keepdims=True)
        base = base + counts[rows, LANES:]
        slot = slot_f.astype(jnp.int32)
        tok = iota((1, LANES), 1) + blk * LANES
        match = slot == slot_ids
        tok_hi = (tok // CHIPS).astype(jnp.float32)
        tok_lo = (tok % CHIPS).astype(jnp.float32)
        high = high + lax.dot_general(hit_b, jnp.where(match, tok_hi, 0.0).astype(jnp.bfloat16), dims, preferred_element_type=jnp.float32)
        low = low + lax.dot_general(hit_b, jnp.where(match, tok_lo, 0.0).astype(jnp.bfloat16), dims, preferred_element_type=jnp.float32)
        e = idx_ref[blk:blk + 1, :]
        dx = ((e & 3) - x) & 3
        dy = (((e >> 2) & 3) - y) & 3
        dz = ((e >> 4) - z) & 3
        side = jnp.where(slot >= half, 1, 0)
        rest = slot - side * half
        unit = rest >> 3
        turn = unit + 2 * side
        turn = turn - jnp.where(turn >= 3, 3, 0) - jnp.where(turn >= 6, 3, 0)
        block = jnp.where(turn == 0, dx * 16 + dy * 4 + dz, jnp.where(turn == 1, dy * 16 + dz * 4 + dx, dz * 16 + dx * 4 + dy))
        place = side * (units * CHIPS * SUB) + unit * (CHIPS * SUB) + block * SUB + (rest & 7)
        place_ref[blk:blk + 1, :] = jnp.where(slot < cap, place, CHIPS * cap)
    table_ref[:, :cap] = (high * CHIPS + low).astype(jnp.int32)


def unit_axes(unit, tp):
    x, y, z = my_coords()
    pairs = ((x, 1), (y, SIDE), (z, SIDE * SIDE))
    out = []
    for k in range(3):
        (c0, s0), (c1, s1) = pairs[(unit + k) % 3], pairs[(unit + 2 + k) % 3]
        out.append((c0 * (1 - tp) + c1 * tp, s0 * (1 - tp) + s1 * tp))
    return out


def spread(x_ref, x3, row0, groups):
    cols = x_ref.shape[-1] // LANES

    def step(g, carry):
        v = x_ref[pl.ds(pl.multiple_of(row0 + g * 16, 16), 16), :].astype(jnp.float32)
        at = (row0 + g * 16) * SUB
        for h in range(2):
            for j in range(cols):
                x3[pl.ds(at + h * SUB * SUB + j, SUB, stride=SUB), :] = v[h * SUB:(h + 1) * SUB, j * LANES:(j + 1) * LANES]
        return carry

    lax.fori_loop(0, groups, step, 0, unroll=2)


def gather_kernel(cap, units, table, act, out, stage, x3, tmp, rows_out, in_sem, out_sem):
    tp = lax.axis_index("tp")
    tokens, hidden = act.shape
    cols = hidden // LANES
    chunk = 512
    n = tokens // chunk
    loads = [pltpu.make_async_copy(act.at[pl.ds(k * chunk, chunk)], stage.at[pl.ds(k * chunk, chunk)], in_sem.at[k]) for k in range(n)]
    for c in loads:
        c.start()
    for k in range(n):
        loads[k].wait()
        spread(stage, x3, k * chunk, chunk // 16)
    stores = []
    for u in range(units):
        (a, sa), (b, sb), (c, sc) = unit_axes(u, tp)

        def step(d, carry):
            e = ((a + d // 16) % SIDE) * sa + ((b + (d // 4) % SIDE) % SIDE) * sb + ((c + d % SIDE) % SIDE) * sc
            at = e * cap + tp * (cap // 2) + u * SUB
            for k in range(SUB):
                i = table[at + k]
                tmp[k * SUB:(k + 1) * SUB, :] = x3[pl.ds(pl.multiple_of(i * SUB, SUB), SUB), :]
            for j in range(cols):
                rows_out[u, d, :, j * LANES:(j + 1) * LANES] = tmp[pl.ds(j, SUB, stride=SUB), :].astype(jnp.bfloat16)
            return carry

        lax.fori_loop(0, CHIPS, step, 0)
        st = pltpu.make_async_copy(rows_out.at[u], out.at[u], out_sem.at[u])
        st.start()
        stores.append(st)
    for st in stores:
        st.wait()


def expert_kernel(units, sent, w_in, w_out, out, b1, b2, b3, r1, r2, own, wi, wo, xb, acc, s_sem, r_sem, w_s, w_r, w_l, l_sem, f_s, f_r, f_l):
    tp = lax.axis_index("tp")
    me = lax.axis_index("ep")
    hidden = xb.shape[1]
    halves = w_in.shape[2] // wi.shape[2]
    width = wi.shape[2]

    def dev(ep, core):
        return (0, core, ep)

    def peer(axis, shift):
        pos, stride = axis
        return dev(me + ((pos + shift) % SIDE - pos) * stride, tp)

    axes = [unit_axes(u, tp) for u in range(units)]
    barrier = pltpu.get_barrier_semaphore()
    for axis in axes[0]:
        for shift in (1, 2, 3):
            pl.semaphore_signal(barrier, inc=1, device_id=peer(axis, shift), device_id_type=MESH)
    pl.semaphore_signal(barrier, inc=1, device_id=dev(me, 1 - tp), device_id_type=MESH)
    pl.semaphore_wait(barrier, 10)

    started = []

    def push(src, dst, send, recv, to):
        copy = pltpu.make_async_remote_copy(src_ref=src, dst_ref=dst, send_sem=send, recv_sem=recv, device_id=to, device_id_type=MESH)
        copy.start()
        started.append(copy)
        return copy

    flights = {}

    def leg(phase, u, axis, sign, src_of, dst_of):
        flights[phase, u] = [
            push(src_of(d), dst_of(d), s_sem.at[phase, u, d - 1], r_sem.at[phase, u, d - 1], peer(axis, sign * d)) for d in (1, 2, 3)
        ]

    def landed(phase, u):
        for copy in flights[phase, u]:
            copy.wait_recv()

    locals_ = [pltpu.make_async_copy(sent.at[u, 0], b1.at[u, 0], l_sem.at[u]) for u in range(units)]

    def d1(u):
        locals_[u].start()
        leg(0, u, axes[u][0], 1, lambda d: sent.at[u, d], lambda d: b1.at[u, d])

    def d2(u):
        locals_[u].wait()
        landed(0, u)
        leg(1, u, axes[u][1], 1, lambda d: b1.at[u, :, d], lambda d: b2.at[u, d])
        b2[u, 0] = b1[u, :, 0]

    def d3(u):
        landed(1, u)
        leg(2, u, axes[u][2], 1, lambda d: b2.at[u, :, :, d], lambda d: b3.at[u, d])
        b3[u, 0] = b2[u, :, :, 0]

    def ffn(u):
        landed(2, u)
        for d in range(SIDE):
            v = b3[u, d].astype(jnp.float32).reshape(SIDE * SIDE * SUB, hidden)
            xb[d * SIDE * SIDE * SUB:(d + 1) * SIDE * SIDE * SUB, :] = v.astype(jnp.bfloat16)

        def step(n, carry):
            pre = jnp.dot(xb[...], wi[n], preferred_element_type=jnp.float32)
            mid = jax.nn.gelu(pre, approximate=True).astype(jnp.bfloat16)
            acc[...] += jnp.dot(mid, wo[n], preferred_element_type=jnp.float32)
            return carry

        acc[...] = jnp.zeros_like(acc)
        lax.fori_loop(0, wi.shape[0], step, 0)
        for d in range(SIDE):
            v = acc[d * SIDE * SIDE * SUB:(d + 1) * SIDE * SIDE * SUB, :]
            b3[u, d] = v.reshape(SIDE, SIDE, SUB, hidden).astype(jnp.bfloat16)

    def q1(u):
        leg(3, u, axes[u][2], -1, lambda d: b3.at[u, d], lambda d: r1.at[u, d])
        r1[u, 0] = b3[u, 0]

    def q2(u):
        landed(3, u)
        leg(4, u, axes[u][1], -1, lambda d: r1.at[u, :, d], lambda d: r2.at[u, d])
        r2[u, 0] = r1[u, :, 0]

    def q3(u):
        landed(4, u)
        leg(5, u, axes[u][0], -1, lambda d: r2.at[u, :, :, d], lambda d: own.at[u, d])
        own[u, 0] = r2[u, :, :, 0]

    finals = []

    def fin(u):
        landed(5, u)
        keep = pltpu.make_async_copy(own.at[u], out.at[tp, u], f_l.at[u])
        keep.start()
        finals.append(keep)
        flights["fin", u] = [push(own.at[u], out.at[tp, u], f_s.at[u], f_r.at[u], dev(me, 1 - tp))]

    weights = []
    for j in range(halves):
        n = tp * halves + j
        for k, (src, dst) in enumerate(((w_in.at[0, :, pl.ds(j * width, width)], wi.at[n]), (w_out.at[0, pl.ds(j * width, width), :], wo.at[n]))):
            copy = pltpu.make_async_copy(src, dst, w_l.at[k, j])
            copy.start()
            weights.append(copy)
            flights["w", k, j] = [push(src, dst, w_s.at[k, j], w_r.at[k, j], dev(me, 1 - tp))]

    for u in (0, 1, 2):
        d1(u)
    for u in (0, 1, 2):
        d2(u)
    for u in (3, 4):
        d1(u)
    for u in (0, 1, 2):
        d3(u)
    for u in (3, 4):
        d2(u)
    for copy in weights:
        copy.wait()
    for k in range(2):
        for j in range(halves):
            for copy in flights["w", k, j]:
                copy.wait_recv()
    ffn(0)
    q1(0)
    for u in (3, 4):
        d3(u)
    ffn(1)
    q1(1)
    ffn(2)
    q1(2)
    q2(0)
    ffn(3)
    q1(3)
    q2(1)
    q3(0)
    ffn(4)
    q1(4)
    q2(2)
    q3(1)
    fin(0)
    q2(3)
    q3(2)
    fin(1)
    q2(4)
    q3(3)
    fin(2)
    q3(4)
    fin(3)
    fin(4)
    for u in range(units):
        for copy in flights["fin", u]:
            copy.wait_recv()
    for copy in finals:
        copy.wait()
    for copy in started:
        copy.wait_send()


def combine_kernel(place, gates, rows, out, stage, x3, tmp, rows_out, in_sem, out_sem):
    total, hidden = rows.shape
    tokens = out.shape[0]
    cols = hidden // LANES
    chunk = 512
    n = total // chunk
    loads = [pltpu.make_async_copy(rows.at[pl.ds(k * chunk, chunk)], stage.at[pl.ds(k * chunk, chunk)], in_sem.at[k]) for k in range(n)]
    for c in loads:
        c.start()
    x3[pl.ds(total * SUB, SUB), :] = jnp.zeros((SUB, LANES), jnp.float32)
    for k in range(n):
        loads[k].wait()
        spread(stage, x3, k * chunk, chunk // 16)
    stores = []
    for c in range(tokens // chunk):

        def step(g, carry):
            t0 = c * chunk + g * 16
            for k in range(16):
                i = place[t0 + k]
                tmp[k * SUB:(k + 1) * SUB, :] = x3[pl.ds(pl.multiple_of(i * SUB, SUB), SUB), :] * gates[t0 + k]
            for j in range(cols):
                top = tmp[pl.ds(j, SUB, stride=SUB), :]
                low = tmp[pl.ds(SUB * SUB + j, SUB, stride=SUB), :]
                rows_out[pl.ds(pl.multiple_of(t0, 16), 16), j * LANES:(j + 1) * LANES] = jnp.concatenate([top, low], axis=0).astype(jnp.bfloat16)
            return carry

        lax.fori_loop(0, chunk // 16, step, 0)
        st = pltpu.make_async_copy(rows_out.at[pl.ds(c * chunk, chunk)], out.at[pl.ds(c * chunk, chunk)], out_sem.at[c])
        st.start()
        stores.append(st)
    for st in stores:
        st.wait()


def solution(mesh):
    tp_size = mesh.shape["tp"]
    vmem = pl.BlockSpec(memory_space=pltpu.VMEM)
    smem = pl.BlockSpec(memory_space=pltpu.SMEM)
    hbm = pl.BlockSpec(memory_space=pl.ANY)
    dma = pltpu.SemaphoreType.DMA

    def local_moe(act_loc, idx_loc, gate_loc, w_in, w_out):
        tokens, hidden = act_loc.shape
        cap = capacity_of(1, tokens, CHIPS, tp_size)
        units = cap // tp_size // SUB
        bf16, f32 = jnp.bfloat16, jnp.float32
        place, table = pl.pallas_call(
            functools.partial(route_kernel, cap, units),
            out_shape=(jax.ShapeDtypeStruct((tokens // LANES, LANES), jnp.int32), jax.ShapeDtypeStruct((CHIPS, cap), jnp.int32)),
            in_specs=[vmem],
            out_specs=(vmem, vmem),
            scratch_shapes=[pltpu.VMEM((tokens // LANES * CHIPS, LANES), bf16)],
            name="route",
        )(idx_loc.reshape(tokens // LANES, LANES))
        sent = pl.pallas_call(
            functools.partial(gather_kernel, cap, units),
            out_shape=jax.ShapeDtypeStruct((units, CHIPS, SUB, hidden), bf16),
            in_specs=[smem, hbm],
            out_specs=hbm,
            scratch_shapes=[
                pltpu.VMEM((tokens, hidden), bf16),
                pltpu.VMEM((tokens * SUB, LANES), f32),
                pltpu.VMEM((SUB * SUB, LANES), f32),
                pltpu.VMEM((units, CHIPS, SUB, hidden), bf16),
                dma((8,)),
                dma((units,)),
            ],
            compiler_params=pltpu.CompilerParams(vmem_limit_bytes=48 << 20),
            name="pick",
        )(table.reshape(-1), act_loc)
        cube = (units, SIDE, SIDE, SIDE, SUB, hidden)
        width = 512
        parts = tp_size * w_in.shape[2] // width
        block_rows = CHIPS * SUB
        returned = pl.pallas_call(
            functools.partial(expert_kernel, units),
            out_shape=jax.ShapeDtypeStruct((tp_size,) + cube, bf16),
            in_specs=[hbm, hbm, hbm],
            out_specs=hbm,
            scratch_shapes=[pltpu.VMEM(cube, bf16)] * 6
            + [
                pltpu.VMEM((parts, hidden, width), bf16),
                pltpu.VMEM((parts, width, hidden), bf16),
                pltpu.VMEM((block_rows, hidden), bf16),
                pltpu.VMEM((block_rows, hidden), f32),
                dma((6, units, 3)),
                dma((6, units, 3)),
                dma((2, parts // tp_size)),
                dma((2, parts // tp_size)),
                dma((2, parts // tp_size)),
                dma((units,)),
                dma((units,)),
                dma((units,)),
                dma((units,)),
            ],
            compiler_params=pltpu.CompilerParams(collective_id=0, has_side_effects=True, vmem_limit_bytes=62 << 20),
            name="expert",
        )(sent.reshape(cube), w_in, w_out)
        total = tp_size * units * block_rows
        return pl.pallas_call(
            combine_kernel,
            out_shape=jax.ShapeDtypeStruct((tokens, hidden), bf16),
            in_specs=[smem, smem, hbm],
            out_specs=hbm,
            scratch_shapes=[
                pltpu.VMEM((total, hidden), bf16),
                pltpu.VMEM(((total + 1) * SUB, LANES), f32),
                pltpu.VMEM((2 * SUB * SUB, LANES), f32),
                pltpu.VMEM((tokens, hidden), bf16),
                dma((total // 512,)),
                dma((tokens // 512,)),
            ],
            compiler_params=pltpu.CompilerParams(vmem_limit_bytes=48 << 20),
            name="combine",
        )(place.reshape(-1), gate_loc.reshape(-1), returned.reshape(total, hidden))

    tok_spec = P(("dp", "ep"), None)
    return jax.shard_map(local_moe, mesh=mesh, in_specs=(tok_spec, tok_spec, tok_spec, P("ep", None, "tp"), P("ep", "tp", None)), out_specs=tok_spec, check_vma=False)
```

time: 361 us -> 171 us (0.47)
  Pallas kernels: 0 us -> 167 us
  blocking collectives: 126 us -> 0 us
  waiting for transfers between devices: 76 us -> 0 us
  local copies, waits for them, and re-layouts: 55.8 us -> 2.76 us
  other arithmetic: 52.1 us -> 0 us
  matrix products: 33.7 us -> 0 us
  between operations: 13.2 us -> 0.05 us
    pallas_call x0 -> x4, Pallas kernels: none -> 167 us  [the longest x1 131 us: local_moe(): pl.pallas_call(functools.partial(expert_kernel, units), out_shape=jax.Sha...]
    all_to_all x2 -> x0, blocking collectives: 126 us -> none  [the longest x1 65.3 us: local_moe(): arrived = lax.all_to_all(outgoing, 'ep', 1, 1, tiled=True)]
    all_gather x2 -> x0, waiting for transfers between devices: 51.2 us -> none  [the longest x1 26.6 us: local_moe(): lax.all_gather(returned, 'tp', axis=2, tiled=True)]
    gather x2 -> x0, local copies, waits for them, and re-layouts: 37.2 us -> none  [the longest x1 23.3 us: local_moe(): picked = jnp.take(own_out, out_pos, axis=0, mode='fill', fill_value=0)]
    another operation x3 -> x0, other arithmetic: 33.8 us -> none
    dot_general x1 -> x0, matrix products: 33.7 us -> none  [local_moe(): jnp.einsum('escf,efd->escd', hidden_act, w_out, preferred_element_type=jn...]
    reduce_scatter x1 -> x0, waiting for transfers between devices: 24.8 us -> none  [local_moe(): lax.psum_scatter(part_out, 'tp', scatter_dimension=2, tiled=True)]
    scatter x1 -> x0, local copies, waits for them, and re-layouts: 15.5 us -> none  [local_moe(): jnp.full((n_send + 1,), tokens, jnp.int32).at[send_pos].set(tok_ids)]
  transfers between devices with their start and end apart: 3 -> 0, of which waited for: 3 -> 0; matrix products, arithmetic and copies ran while one was open for 0% -> 0% of each run, Pallas kernels for 0% -> 0%
where the time goes in v1:
time: 171 us; the launch traced here: 170 us
  Pallas kernels  167 us (98%)
  local copies, waits for them, and re-layouts  2.76 us (2%)
    pallas_call x1, Pallas kernels, local_moe(): pl.pallas_call(functools.partial(expert_kernel, units), out_shape=jax.Sha...  131 us
    pallas_call x1, Pallas kernels, local_moe(): pl.pallas_call(functools.partial(gather_kernel, cap, units), out_shape=ja...  18.4 us
    pallas_call x1, Pallas kernels, local_moe(): pl.pallas_call(combine_kernel, out_shape=jax.ShapeDtypeStruct((tokens, hi...  15.1 us

profile of v1, /device:TPU:41, one launch (start us, length us, event | category | flops | bytes accessed | tf_op | source)
XLA Modules:
  0.0 170.3 jit_solution(6981891682595271711)
XLA Ops:
  0.0 2.7 %route.1 = (s32[32,128]{1,0:T(8,128)}, s32[64,80]{1,0:T(8,128)}) custom-call(s32[32,128]{1,0:T(8,128)} %bitcast.9), custom_call_target="tpu_custom_call" | custom-call | tf_op jit(solution)/shard_map/route/pallas_call | solution.py:340
  2.7 0.8 reshape.21.table
  3.6 18.4 %pick.1 = bf16[5,64,8,768]{3,2,1,0:T(8,128)(2,1)S(1)} custom-call(s32[5120]{0:T(1024)S(1)} %reshape.21.table, bf16[4096,768]{1,0:T(8,128)(2,1)} %act.1), custom_call_target="tpu_custom_call" | custom-call | tf_op jit(solution)/shard_map/pick/pallas_call | solution.py:348
  22.0 0.0 copy-start
  22.0 1.9 %copy-done = bf16[5,64,8,768]{3,2,1,0:T(8,128)(2,1)} copy-done((bf16[5,64,8,768]{3,2,1,0:T(8,128)(2,1)}, bf16[5,64,8,768]{3,2,1,0:T(8,128)(2,1)S(1)}, u32[]{:S(2)}) %copy-start) | copy-done | bytes 3932184
  23.9 0.0 copy-start.1
  23.9 0.0 copy-start.2
  23.9 131.2 %expert.1 = bf16[2,5,4,4,4,8,768]{6,5,4,3,2,1,0:T(8,128)(2,1)} custom-call(bf16[5,4,4,4,8,768]{5,4,3,2,1,0:T(8,128)(2,1)} %bitcast.5, bf16[1,768,1536]{2,1,0:T(8,128)(2,1)} %w_in.1, bf16[1,1536,768]{2,1,0:T(8,128)(2,1)} %w_out.1), custom_call_target="tpu_custom_call" | custom-call | tf_op jit(solution)/shard_map/expert/pallas_call | solution.py:368
  155.1 0.0 copy-done.1
  155.1 0.0 copy-done.2
  155.2 15.1 %combine.1 = bf16[4096,768]{1,0:T(8,128)(2,1)} custom-call(s32[4096]{0:T(1024)S(1)} %bitcast.7, f32[4096]{0:T(1024)S(1)} %bitcast.6, bf16[5120,768]{1,0:T(8,128)(2,1)} %bitcast.8), custom_call_target="tpu_custom_call" | custom-call | tf_op jit(solution)/shard_map/combine/pallas_call | solution.py:393
Async XLA Ops:
  22.0 1.9 %copy-start = (bf16[5,64,8,768]{3,2,1,0:T(8,128)(2,1)}, bf16[5,64,8,768]{3,2,1,0:T(8,128)(2,1)S(1)}, u32[]{:S(2)}) copy-start(bf16[5,64,8,768]{3,2,1,0:T(8,128)(2,1)S(1)} %pick.1) | copy-start | bytes 11796484
  23.9 131.2 %copy-start.1 = (f32[4096,1]{0,1:T(1,128)S(1)}, f32[4096,1]{0,1:T(1,128)}, u32[]{:S(2)}) copy-start(f32[4096,1]{0,1:T(1,128)} %param.7) | copy-start | bytes 49156
  23.9 131.2 %copy-start.2 = (s32[32,128]{1,0:T(8,128)S(1)}, s32[32,128]{1,0:T(8,128)}, u32[]{:S(2)}) copy-start(s32[32,128]{1,0:T(8,128)} %get-tuple-element.7) | copy-start | bytes 49156

commit v2 on v1

v2 whole, which is shorter than its diff:
```python
import functools

import jax
import jax.numpy as jnp
from jax import lax
from jax.experimental import pallas as pl
from jax.experimental.pallas import tpu as pltpu
from jax.sharding import PartitionSpec as P

MESH = pl.DeviceIdType.MESH
SIDE = 4
CHIPS = SIDE ** 3
SUB = 8
LANES = 128
PITCH = 6
ORDER = "a0 a2 a4 a1 b0 a3 b1 c0 b3 b2 w b4 c1 g0 c2 h0 x0 g1 c4 c3 h1 y0 x1 g2 h2 g3 x2 z0 y1 h3 g4 x3 h4 x4 z1 y3 y2 y4 z2 z4 z3 e2 e0 e1 e3 e4"


def capacity_of(top_k, tokens, experts, tp_size):
    divisor = 32 * experts * tp_size
    return 8 * tp_size * ((5 * top_k * tokens + divisor - 1) // divisor)


def my_coords():
    me = lax.axis_index("ep")
    return me % SIDE, (me // SIDE) % SIDE, me // (SIDE * SIDE)


def iota(shape, dim):
    return lax.broadcasted_iota(jnp.int32, shape, dim)


def route_kernel(cap, units, idx_ref, place_ref, table_ref, hits):
    blocks = idx_ref.shape[0]
    half = cap // 2
    expert_ids = iota((CHIPS, LANES), 0)
    for blk in range(blocks):
        hit = idx_ref[blk:blk + 1, :] == expert_ids
        hits[blk * CHIPS:(blk + 1) * CHIPS, :] = jnp.where(hit, 1.0, 0.0).astype(jnp.bfloat16)
    before = jnp.where(iota((LANES, LANES), 0) < iota((LANES, LANES), 1), 1.0, 0.0)
    mix = jnp.concatenate([before, jnp.ones((LANES, LANES), jnp.float32)], axis=1).astype(jnp.bfloat16)
    counts = jnp.dot(hits[...], mix, preferred_element_type=jnp.float32)
    base = jnp.zeros((CHIPS, LANES), jnp.float32)
    x, y, z = my_coords()
    high = jnp.zeros((CHIPS, cap), jnp.float32)
    low = jnp.zeros((CHIPS, cap), jnp.float32)
    slot_ids = iota((cap, LANES), 0)
    dims = (((1,), (1,)), ((), ()))
    for blk in range(blocks):
        rows = slice(blk * CHIPS, (blk + 1) * CHIPS)
        hit_b = hits[rows, :]
        rank = counts[rows, :LANES] + base
        slot_f = jnp.sum(hit_b.astype(jnp.float32) * rank, axis=0, keepdims=True)
        base = base + counts[rows, LANES:]
        slot = slot_f.astype(jnp.int32)
        tok = iota((1, LANES), 1) + blk * LANES
        match = slot == slot_ids
        tok_hi = (tok // CHIPS).astype(jnp.float32)
        tok_lo = (tok % CHIPS).astype(jnp.float32)
        high = high + lax.dot_general(hit_b, jnp.where(match, tok_hi, 0.0).astype(jnp.bfloat16), dims, preferred_element_type=jnp.float32)
        low = low + lax.dot_general(hit_b, jnp.where(match, tok_lo, 0.0).astype(jnp.bfloat16), dims, preferred_element_type=jnp.float32)
        e = idx_ref[blk:blk + 1, :]
        dx = ((e & 3) - x) & 3
        dy = (((e >> 2) & 3) - y) & 3
        dz = ((e >> 4) - z) & 3
        side = jnp.where(slot >= half, 1, 0)
        rest = slot - side * half
        unit = rest >> 3
        turn = unit + 2 * side
        turn = turn - jnp.where(turn >= 3, 3, 0) - jnp.where(turn >= 6, 3, 0)
        block = jnp.where(turn == 0, dx * 16 + dy * 4 + dz, jnp.where(turn == 1, dy * 16 + dz * 4 + dx, dz * 16 + dx * 4 + dy))
        place = side * (units * CHIPS * SUB) + unit * (CHIPS * SUB) + block * SUB + (rest & 7)
        place_ref[blk:blk + 1, :] = jnp.where(slot < cap, place, CHIPS * cap) * PITCH
    table_ref[...] = (high * CHIPS + low).astype(jnp.int32) * PITCH


def unit_axes(unit, tp):
    x, y, z = my_coords()
    pairs = ((x, 1), (y, SIDE), (z, SIDE * SIDE))
    out = []
    for k in range(3):
        (c0, s0), (c1, s1) = pairs[(unit + k) % 3], pairs[(unit + 2 + k) % 3]
        out.append((c0 * (1 - tp) + c1 * tp, s0 * (1 - tp) + s1 * tp))
    return out


def spread(x_ref, x3, src0, dst0, groups):
    cols = x_ref.shape[-1] // LANES

    def step(g, carry):
        v = x_ref[pl.ds(pl.multiple_of(src0 + g * 16, 16), 16), :].astype(jnp.float32)
        at = (dst0 + g * 16) * PITCH
        for h in range(2):
            for j in range(cols):
                x3[pl.ds(at + h * SUB * PITCH + j, SUB, stride=PITCH), :] = v[h * SUB:(h + 1) * SUB, j * LANES:(j + 1) * LANES]
        return carry

    lax.fori_loop(0, groups, step, 0, unroll=4)


def expert_kernel(cap, units, table, act, w_in, w_out, out, stage, x3, tmp, sent, b1, b2, b3, r1, r2, own, wi, wo, xb, acc, a_sem, s_sem, r_sem, w_s, w_r, w_l, f_s, f_r, f_l):
    tp = lax.axis_index("tp")
    me = lax.axis_index("ep")
    hidden = xb.shape[1]
    cols = hidden // LANES
    slots, chunk = stage.shape[:2]
    pieces = act.shape[0] // chunk
    tall = SIDE * SIDE * SUB
    loads = [pltpu.make_async_copy(act.at[pl.ds(k * chunk, chunk)], stage.at[k % slots], a_sem.at[k]) for k in range(pieces)]
    for copy in loads[:slots]:
        copy.start()

    def dev(ep, core):
        return (0, core, ep)

    def peer(axis, shift):
        pos, stride = axis
        return dev(me + ((pos + shift) % SIDE - pos) * stride, tp)

    axes = [unit_axes(u, tp) for u in range(units)]
    barrier = pltpu.get_barrier_semaphore()
    for axis in axes[0]:
        for shift in (1, 2, 3):
            pl.semaphore_signal(barrier, inc=1, device_id=peer(axis, shift), device_id_type=MESH)
    pl.semaphore_signal(barrier, inc=1, device_id=dev(me, 1 - tp), device_id_type=MESH)
    for k in range(pieces):
        loads[k].wait()
        spread(stage.at[k % slots], x3, 0, k * chunk, chunk // 16)
        if k + slots < pieces:
            loads[k + slots].start()
    pl.semaphore_wait(barrier, 10)

    started = []

    def push(src, dst, send, recv, to):
        copy = pltpu.make_async_remote_copy(src_ref=src, dst_ref=dst, send_sem=send, recv_sem=recv, device_id=to, device_id_type=MESH)
        copy.start()
        started.append(copy)
        return copy

    flights = {}

    def leg(phase, u, axis, sign, src_of, dst_of):
        flights[phase, u] = [
            push(src_of(d), dst_of(d), s_sem.at[phase, u, d - 1], r_sem.at[phase, u, d - 1], peer(axis, sign * d)) for d in (1, 2, 3)
        ]

    def landed(phase, u):
        for copy in flights[phase, u]:
            copy.wait_recv()

    def pick(u, shift, target):
        (a, sa), (b, sb), (c, sc) = axes[u]

        def step(db, carry):
            rows = []
            for dc in range(SIDE):
                e = ((a + shift) % SIDE) * sa + ((b + db) % SIDE) * sb + ((c + dc) % SIDE) * sc
                at = tp * (cap // 2) + u * SUB
                rows += [x3[pl.ds(table[e, at + k], SUB), :] for k in range(SUB)]
            for k, row in enumerate(rows):
                tmp[k * SUB:(k + 1) * SUB, :] = row
            for dc in range(SIDE):
                for j in range(cols):
                    target[db, dc, :, j * LANES:(j + 1) * LANES] = tmp[pl.ds(dc * SUB * SUB + j, SUB, stride=SUB), :].astype(jnp.bfloat16)
            return carry

        lax.fori_loop(0, SIDE, step, 0, unroll=2)

    def d1(u):
        for shift in range(1, SIDE):
            pick(u, shift, sent.at[u, shift - 1])
        leg(0, u, axes[u][0], 1, lambda d: sent.at[u, d - 1], lambda d: b1.at[u, d])
        pick(u, 0, b1.at[u, 0])

    def d2(u):
        landed(0, u)
        leg(1, u, axes[u][1], 1, lambda d: b1.at[u, :, d], lambda d: b2.at[u, d])
        b2[u, 0] = b1[u, :, 0]

    def d3(u):
        landed(1, u)
        leg(2, u, axes[u][2], 1, lambda d: b2.at[u, :, :, d], lambda d: b3.at[u, d])
        b3[u, 0] = b2[u, :, :, 0]

    def half(u, n, d):
        rows = slice(d * tall, (d + 1) * tall)
        pre = jnp.dot(xb[rows, :], wi[n], preferred_element_type=jnp.float32)
        mid = jax.nn.gelu(pre, approximate=True).astype(jnp.bfloat16)
        return jnp.dot(mid, wo[n], preferred_element_type=jnp.float32)

    def first(u):
        landed(2, u)
        for d in range(SIDE):
            rows = slice(d * tall, (d + 1) * tall)
            xb[rows, :] = b3[u, d].astype(jnp.float32).reshape(tall, hidden).astype(jnp.bfloat16)
        for d in range(SIDE):
            acc[d * tall:(d + 1) * tall, :] = half(u, 0, d)

    def second(u):
        for d in range(SIDE):
            total = acc[d * tall:(d + 1) * tall, :] + half(u, 1, d)
            b3[u, d] = total.reshape(SIDE, SIDE, SUB, hidden).astype(jnp.bfloat16)

    def q1(u):
        leg(3, u, axes[u][2], -1, lambda d: b3.at[u, d], lambda d: r1.at[u, d])
        r1[u, 0] = b3[u, 0]

    def q2(u):
        landed(3, u)
        leg(4, u, axes[u][1], -1, lambda d: r1.at[u, :, d], lambda d: r2.at[u, d])
        r2[u, 0] = r1[u, :, 0]

    def q3(u):
        landed(4, u)
        leg(5, u, axes[u][0], -1, lambda d: r2.at[u, :, :, d], lambda d: own.at[u, d])
        own[u, 0] = r2[u, :, :, 0]

    finals = []

    def fin(u):
        landed(5, u)
        keep = pltpu.make_async_copy(own.at[u], out.at[tp, u], f_l.at[u])
        keep.start()
        finals.append(keep)
        flights["fin", u] = [push(own.at[u], out.at[tp, u], f_s.at[u], f_r.at[u], dev(me, 1 - tp))]

    weights = []
    for k, (src, dst) in enumerate(((w_in.at[0], wi.at[tp]), (w_out.at[0], wo.at[tp]))):
        copy = pltpu.make_async_copy(src, dst, w_l.at[k])
        copy.start()
        weights.append(copy)
        flights["w", k] = [push(src, dst, w_s.at[k], w_r.at[k], dev(me, 1 - tp))]

    def ready():
        for copy in weights:
            copy.wait()
        for k in range(2):
            for copy in flights["w", k]:
                copy.wait_recv()

    ops = {"a": d1, "b": d2, "c": d3, "g": first, "h": second, "x": q1, "y": q2, "z": q3, "e": fin}
    for word in ORDER.split():
        if word == "w":
            ready()
        else:
            ops[word[0]](int(word[1]))
    for u in range(units):
        for copy in flights["fin", u]:
            copy.wait_recv()
    for copy in finals:
        copy.wait()
    for copy in started:
        copy.wait_send()


def combine_kernel(place, gates, rows, out, stage, x3, tmp, scale, rows_out, in_sem, out_sem):
    total, hidden = rows.shape
    tokens = out.shape[0]
    cols = hidden // LANES
    chunk = 512
    n = total // chunk
    loads = [pltpu.make_async_copy(rows.at[pl.ds(k * chunk, chunk)], stage.at[pl.ds(k * chunk, chunk)], in_sem.at[k]) for k in range(n)]
    for c in loads:
        c.start()
    x3[pl.ds(total * PITCH, SUB), :] = jnp.zeros((SUB, LANES), jnp.float32)
    for k in range(tokens // LANES):
        scale[k * LANES:(k + 1) * LANES, :] = jnp.transpose(jnp.broadcast_to(gates[k:k + 1, :], (LANES, LANES)))
    for k in range(n):
        loads[k].wait()
        spread(stage, x3, k * chunk, k * chunk, chunk // 16)
    stores = []
    for c in range(tokens // chunk):

        def step(g, carry):
            t0 = c * chunk + g * 32
            picked = [x3[pl.ds(place[t0 + k], SUB), :] for k in range(32)]
            for k, row in enumerate(picked):
                tmp[k * SUB:(k + 1) * SUB, :] = row
            for h in range(2):
                gate_a = scale[pl.ds(pl.multiple_of(t0 + h * 16, SUB), SUB), :]
                gate_b = scale[pl.ds(pl.multiple_of(t0 + h * 16 + SUB, SUB), SUB), :]
                for j in range(cols):
                    top = tmp[pl.ds(2 * h * SUB * SUB + j, SUB, stride=SUB), :] * gate_a
                    low = tmp[pl.ds((2 * h + 1) * SUB * SUB + j, SUB, stride=SUB), :] * gate_b
                    rows_out[pl.ds(pl.multiple_of(t0 + h * 16, 16), 16), j * LANES:(j + 1) * LANES] = jnp.concatenate([top, low], axis=0).astype(jnp.bfloat16)
            return carry

        lax.fori_loop(0, chunk // 32, step, 0, unroll=2)
        st = pltpu.make_async_copy(rows_out.at[pl.ds(c * chunk, chunk)], out.at[pl.ds(c * chunk, chunk)], out_sem.at[c])
        st.start()
        stores.append(st)
    for st in stores:
        st.wait()


def solution(mesh):
    tp_size = mesh.shape["tp"]
    vmem = pl.BlockSpec(memory_space=pltpu.VMEM)
    smem = pl.BlockSpec(memory_space=pltpu.SMEM)
    hbm = pl.BlockSpec(memory_space=pl.ANY)
    dma = pltpu.SemaphoreType.DMA

    def local_moe(act_loc, idx_loc, gate_loc, w_in, w_out):
        tokens, hidden = act_loc.shape
        cap = capacity_of(1, tokens, CHIPS, tp_size)
        units = cap // tp_size // SUB
        bf16, f32 = jnp.bfloat16, jnp.float32
        place, table = pl.pallas_call(
            functools.partial(route_kernel, cap, units),
            out_shape=(jax.ShapeDtypeStruct((tokens // LANES, LANES), jnp.int32), jax.ShapeDtypeStruct((CHIPS, cap), jnp.int32)),
            in_specs=[vmem],
            out_specs=(vmem, vmem),
            scratch_shapes=[pltpu.VMEM((tokens // LANES * CHIPS, LANES), bf16)],
            name="route",
        )(idx_loc.reshape(tokens // LANES, LANES))
        cube = (units, SIDE, SIDE, SIDE, SUB, hidden)
        width = w_in.shape[2]
        block_rows = CHIPS * SUB
        chunk = 512
        returned = pl.pallas_call(
            functools.partial(expert_kernel, cap, units),
            out_shape=jax.ShapeDtypeStruct((tp_size,) + cube, bf16),
            in_specs=[smem, hbm, hbm, hbm],
            out_specs=hbm,
            scratch_shapes=[
                pltpu.VMEM((4, chunk, hidden), bf16),
                pltpu.VMEM((tokens * PITCH + SUB, LANES), f32),
                pltpu.VMEM((SIDE * SUB * SUB, LANES), f32),
                pltpu.VMEM((units, SIDE - 1) + cube[2:], bf16),
            ]
            + [pltpu.VMEM(cube, bf16)] * 6
            + [
                pltpu.VMEM((tp_size, hidden, width), bf16),
                pltpu.VMEM((tp_size, width, hidden), bf16),
                pltpu.VMEM((block_rows, hidden), bf16),
                pltpu.VMEM((block_rows, hidden), f32),
                dma((tokens // chunk,)),
                dma((6, units, 3)),
                dma((6, units, 3)),
                dma((2,)),
                dma((2,)),
                dma((2,)),
                dma((units,)),
                dma((units,)),
                dma((units,)),
            ],
            compiler_params=pltpu.CompilerParams(collective_id=0, has_side_effects=True, vmem_limit_bytes=67043328),
            name="expert",
        )(table, act_loc, w_in, w_out)
        total = tp_size * units * block_rows
        return pl.pallas_call(
            combine_kernel,
            out_shape=jax.ShapeDtypeStruct((tokens, hidden), bf16),
            in_specs=[smem, vmem, hbm],
            out_specs=hbm,
            scratch_shapes=[
                pltpu.VMEM((total, hidden), bf16),
                pltpu.VMEM((total * PITCH + SUB, LANES), f32),
                pltpu.VMEM((4 * SUB * SUB, LANES), f32),
                pltpu.VMEM((tokens, LANES), f32),
                pltpu.VMEM((tokens, hidden), bf16),
                dma((total // 512,)),
                dma((tokens // 512,)),
            ],
            compiler_params=pltpu.CompilerParams(vmem_limit_bytes=48 << 20),
            name="combine",
        )(place.reshape(-1), gate_loc.reshape(tokens // LANES, LANES), returned.reshape(total, hidden))

    tok_spec = P(("dp", "ep"), None)
    return jax.shard_map(local_moe, mesh=mesh, in_specs=(tok_spec, tok_spec, tok_spec, P("ep", None, "tp"), P("ep", "tp", None)), out_specs=tok_spec, check_vma=False)
```

time: 171 us -> 135 us (0.79)
  the two profiles are of different devices: /device:TPU:41 before, /device:TPU:35 now
where the time goes in v2:
time: 135 us
  Pallas kernels  133 us (99%)
  local copies, waits for them, and re-layouts  1.43 us (1%)
    pallas_call x1, Pallas kernels, local_moe(): pl.pallas_call(functools.partial(expert_kernel, cap, units), out_shape=ja...  119 us
    pallas_call x1, Pallas kernels, local_moe(): pl.pallas_call(combine_kernel, out_shape=jax.ShapeDtypeStruct((tokens, hi...  11.2 us
    pallas_call x1, Pallas kernels, local_moe(): pl.pallas_call(functools.partial(route_kernel, cap, units), out_shape=(ja...  2.73 us

profile of v2, /device:TPU:35, one launch (start us, length us, event | category | flops | bytes accessed | tf_op | source)
XLA Modules:
  0.0 134.8 jit_solution(15498096541824274666)
XLA Ops:
  0.0 2.7 %route.1 = (s32[32,128]{1,0:T(8,128)}, s32[64,80]{1,0:T(8,128)}) custom-call(s32[32,128]{1,0:T(8,128)} %bitcast.7), custom_call_target="tpu_custom_call" | custom-call | tf_op jit(solution)/shard_map/route/pallas_call | solution.py:309
  2.7 119.3 %expert.1 = bf16[2,5,4,4,4,8,768]{6,5,4,3,2,1,0:T(8,128)(2,1)} custom-call(s32[64,80]{1,0:T(8,128)} %get-tuple-element.8.table, bf16[4096,768]{1,0:T(8,128)(2,1)} %act.1, bf16[1,768,1536]{2,1,0:T(8,128)(2,1)} %w_in.1, bf16[1,1536,768]{2,1,0:T(8,128)(2,1)} %w_out.1), custom_call_target="tpu_custom_call" | custom-call | tf_op jit(solution)/shard_map/expert/pallas_call | solution.py:321
  122.0 0.0 copy-start
  122.0 0.7 copy-done
  122.7 0.0 copy-start.1
  122.8 0.7 copy-done.1
  123.5 11.2 %combine.1 = bf16[4096,768]{1,0:T(8,128)(2,1)} custom-call(s32[4096]{0:T(1024)S(1)} %bitcast.5, f32[32,128]{1,0:T(8,128)S(1)} %bitcast.4, bf16[5120,768]{1,0:T(8,128)(2,1)} %bitcast.6), custom_call_target="tpu_custom_call" | custom-call | tf_op jit(solution)/shard_map/combine/pallas_call | solution.py:352
Async XLA Ops:
  122.0 0.7 copy-start
  122.7 0.7 copy-start.1

commit v3 on v2

--- a/solution.py
+++ b/solution.py
@@ -13,7 +13,12 @@
 SUB = 8
 LANES = 128
 PITCH = 6
-ORDER = "a0 a2 a4 a1 b0 a3 b1 c0 b3 b2 w b4 c1 g0 c2 h0 x0 g1 c4 c3 h1 y0 x1 g2 h2 g3 x2 z0 y1 h3 g4 x3 h4 x4 z1 y3 y2 y4 z2 z4 z3 e2 e0 e1 e3 e4"
+ORDER = (
+    "a0", "a2", "a1", "a3", "b0", "w", "b2", "b1", "a4", "c0", "c1", "b3",
+    "b4", "c2", "g0", "h0", "x0", "g1", "h1", "c3", "x1", "c4", "g2", "y0",
+    "h2", "x2", "y1", "g3", "h3", "x3", "z0", "g4", "h4", "x4", "z1", "y4",
+    "y2", "y3", "e1", "z4", "z2", "z3", "e2", "e3", "e4", "e0",
+)
 
 
 def capacity_of(top_k, tokens, experts, tp_size):
@@ -240,7 +245,7 @@
                 copy.wait_recv()
 
     ops = {"a": d1, "b": d2, "c": d3, "g": first, "h": second, "x": q1, "y": q2, "z": q3, "e": fin}
-    for word in ORDER.split():
+    for word in ORDER:
         if word == "w":
             ready()
         else:

time: 135 us -> 130 us (0.963)
  the two profiles are of different devices: /device:TPU:35 before, /device:TPU:41 now
where the time goes in v3:
time: 130 us
  Pallas kernels  128 us (98%)
  local copies, waits for them, and re-layouts  1.43 us (1%)
    pallas_call x1, Pallas kernels, local_moe(): pl.pallas_call(functools.partial(expert_kernel, cap, units), out_shape=ja...  114 us
    pallas_call x1, Pallas kernels, local_moe(): pl.pallas_call(combine_kernel, out_shape=jax.ShapeDtypeStruct((tokens, hi...  11.2 us
    pallas_call x1, Pallas kernels, local_moe(): pl.pallas_call(functools.partial(route_kernel, cap, units), out_shape=(ja...  2.73 us

profile of v3, /device:TPU:41, one launch (start us, length us, event | category | flops | bytes accessed | tf_op | source)
XLA Modules:
  0.0 129.9 jit_solution(15999138708330523005)
XLA Ops:
  0.0 2.7 %route.1 = (s32[32,128]{1,0:T(8,128)}, s32[64,80]{1,0:T(8,128)}) custom-call(s32[32,128]{1,0:T(8,128)} %bitcast.7), custom_call_target="tpu_custom_call" | custom-call | tf_op jit(solution)/shard_map/route/pallas_call | solution.py:314
  2.7 114.4 %expert.1 = bf16[2,5,4,4,4,8,768]{6,5,4,3,2,1,0:T(8,128)(2,1)} custom-call(s32[64,80]{1,0:T(8,128)} %get-tuple-element.8.table, bf16[4096,768]{1,0:T(8,128)(2,1)} %act.1, bf16[1,768,1536]{2,1,0:T(8,128)(2,1)} %w_in.1, bf16[1,1536,768]{2,1,0:T(8,128)(2,1)} %w_out.1), custom_call_target="tpu_custom_call" | custom-call | tf_op jit(solution)/shard_map/expert/pallas_call | solution.py:326
  117.1 0.0 copy-start
  117.1 0.7 copy-done
  117.8 0.0 copy-start.1
  117.8 0.7 copy-done.1
  118.5 11.2 %combine.1 = bf16[4096,768]{1,0:T(8,128)(2,1)} custom-call(s32[4096]{0:T(1024)S(1)} %bitcast.5, f32[32,128]{1,0:T(8,128)S(1)} %bitcast.4, bf16[5120,768]{1,0:T(8,128)(2,1)} %bitcast.6), custom_call_target="tpu_custom_call" | custom-call | tf_op jit(solution)/shard_map/combine/pallas_call | solution.py:357
Async XLA Ops:
  117.1 0.7 copy-start
  117.8 0.7 copy-start.1

commit v4 on v3

--- a/solution.py
+++ b/solution.py
@@ -259,16 +259,19 @@
         copy.wait_send()
 
 
-def combine_kernel(place, gates, rows, out, stage, x3, tmp, scale, rows_out, in_sem, out_sem):
+def combine_kernel(place, gates_hbm, rows, out, stage, x3, tmp, gates, scale, rows_out, gate_sem, in_sem, out_sem):
     total, hidden = rows.shape
     tokens = out.shape[0]
     cols = hidden // LANES
     chunk = 512
     n = total // chunk
     loads = [pltpu.make_async_copy(rows.at[pl.ds(k * chunk, chunk)], stage.at[pl.ds(k * chunk, chunk)], in_sem.at[k]) for k in range(n)]
+    gate_load = pltpu.make_async_copy(gates_hbm, gates, gate_sem)
+    gate_load.start()
     for c in loads:
         c.start()
     x3[pl.ds(total * PITCH, SUB), :] = jnp.zeros((SUB, LANES), jnp.float32)
+    gate_load.wait()
     for k in range(tokens // LANES):
         scale[k * LANES:(k + 1) * LANES, :] = jnp.transpose(jnp.broadcast_to(gates[k:k + 1, :], (LANES, LANES)))
     for k in range(n):
@@ -357,18 +360,20 @@
         return pl.pallas_call(
             combine_kernel,
             out_shape=jax.ShapeDtypeStruct((tokens, hidden), bf16),
-            in_specs=[smem, vmem, hbm],
+            in_specs=[smem, hbm, hbm],
             out_specs=hbm,
             scratch_shapes=[
                 pltpu.VMEM((total, hidden), bf16),
                 pltpu.VMEM((total * PITCH + SUB, LANES), f32),
                 pltpu.VMEM((4 * SUB * SUB, LANES), f32),
+                pltpu.VMEM((tokens // LANES, LANES), f32),
                 pltpu.VMEM((tokens, LANES), f32),
                 pltpu.VMEM((tokens, hidden), bf16),
+                dma,
                 dma((total // 512,)),
                 dma((tokens // 512,)),
             ],
-            compiler_params=pltpu.CompilerParams(vmem_limit_bytes=48 << 20),
+            compiler_params=pltpu.CompilerParams(vmem_limit_bytes=67043328),
             name="combine",
         )(place.reshape(-1), gate_loc.reshape(tokens // LANES, LANES), returned.reshape(total, hidden))
 

time: 130 us -> 130 us (level)
  local copies, waits for them, and re-layouts: 1.43 us -> 0 us
    unnamed x4 -> x0, local copies, waits for them, and re-layouts: 1.43 us -> none
where the time goes in v4:
time: 130 us
  Pallas kernels  129 us (99%)
    pallas_call x1, Pallas kernels, local_moe(): pl.pallas_call(functools.partial(expert_kernel, cap, units), out_shape=ja...  114 us
    pallas_call x1, Pallas kernels, local_moe(): pl.pallas_call(combine_kernel, out_shape=jax.ShapeDtypeStruct((tokens, hi...  12.3 us
    pallas_call x1, Pallas kernels, local_moe(): pl.pallas_call(functools.partial(route_kernel, cap, units), out_shape=(ja...  2.73 us

profile of v4, /device:TPU:41, one launch (start us, length us, event | category | flops | bytes accessed | tf_op | source)
XLA Modules:
  0.0 129.6 jit_solution(3973096228431238112)
XLA Ops:
  0.0 2.7 %route.1 = (s32[32,128]{1,0:T(8,128)}, s32[64,80]{1,0:T(8,128)}) custom-call(s32[32,128]{1,0:T(8,128)} %bitcast.7), custom_call_target="tpu_custom_call" | custom-call | tf_op jit(solution)/shard_map/route/pallas_call | solution.py:317
  2.7 114.4 %expert.1 = bf16[2,5,4,4,4,8,768]{6,5,4,3,2,1,0:T(8,128)(2,1)} custom-call(s32[64,80]{1,0:T(8,128)} %get-tuple-element.8.table, bf16[4096,768]{1,0:T(8,128)(2,1)} %act.1, bf16[1,768,1536]{2,1,0:T(8,128)(2,1)} %w_in.1, bf16[1,1536,768]{2,1,0:T(8,128)(2,1)} %w_out.1), custom_call_target="tpu_custom_call" | custom-call | tf_op jit(solution)/shard_map/expert/pallas_call | solution.py:329
  117.1 12.3 %combine.1 = bf16[4096,768]{1,0:T(8,128)(2,1)} custom-call(s32[4096]{0:T(1024)} %bitcast.6, f32[32,128]{1,0:T(8,128)} %bitcast.5, bf16[5120,768]{1,0:T(8,128)(2,1)} %bitcast.4), custom_call_target="tpu_custom_call" | custom-call | tf_op jit(solution)/shard_map/combine/pallas_call | solution.py:360
